TPU v7x, 128 devices: a whole 4x4x4 slice. The times are simulated.
128 devices in a mesh: dp: 1, vp: 128 (over z, y, x, core).
Axes of the slice: x: 4, y: 4, z: 4, core: 2. Of those that a mesh axis runs over, the one named last changes fastest.
Arguments:
- hidden: bfloat16 [2048, 12288], P('dp')
- w_head: bfloat16 [12288, 32768], P(None, 'vp')
- inv_temp: float32 [2048], P('dp')
- target_ids: int32 [2048], P('dp')
Outputs:
- output 1: float32 [2048, 32768], P(('dp', 'vp'))
- output 2: float32 [2048], P('dp')
All inputs are finite; a program needn't handle non-finite values.
Results may differ from a plain program's by a relative error of at most 0.001.
Values are sent between devices in bfloat16 or wider.
A program may use at most 1 GiB of HBM per device.

v0:
```python
import jax
import jax.numpy as jnp
from jax import lax
from jax.sharding import PartitionSpec as P, NamedSharding


def solution(mesh):
    group_size = mesh.shape["vp"]

    def local_step(hidden, w_local, inv_temp, target_ids):
        group_index = lax.axis_index("vp")
        local_vocab = w_local.shape[1]
        logits = jnp.dot(hidden, w_local, preferred_element_type=jnp.float32)
        scaled = logits * inv_temp[:, None]
        local_max = jnp.max(scaled, axis=1)
        exp_vals = jnp.exp(scaled - local_max[:, None])
        local_sum = jnp.sum(exp_vals, axis=1)
        shard_stats = lax.all_gather(jnp.stack([local_max, local_sum]), "vp")
        global_max = jnp.max(shard_stats[:, 0], axis=0)
        global_sum = jnp.sum(shard_stats[:, 1] * jnp.exp(shard_stats[:, 0] - global_max[None, :]), axis=0)
        row_scale = jnp.exp(local_max - global_max) / global_sum
        local_cdf = jnp.cumsum(exp_vals * row_scale[:, None], axis=1)
        totals = lax.all_gather(local_cdf[:, -1], "vp")
        earlier = (jnp.arange(group_size) < group_index)[:, None]
        offset = jnp.sum(jnp.where(earlier, totals, 0.0), axis=0)
        cdf_cols = local_cdf + offset[:, None]
        local_ids = target_ids - group_index * local_vocab
        in_shard = (local_ids >= 0) & (local_ids < local_vocab)
        picked = jnp.take_along_axis(cdf_cols, jnp.clip(local_ids, 0, local_vocab - 1)[:, None], axis=1)[:, 0]
        cdf_at_target = lax.psum(jnp.where(in_shard, picked, 0.0), "vp")
        cdf_rows = lax.all_to_all(cdf_cols, "vp", 0, 1, tiled=True)
        return cdf_rows, cdf_at_target

    return jax.shard_map(
        local_step,
        mesh=mesh,
        in_specs=(P("dp", None), P(None, "vp"), P("dp"), P("dp")),
        out_specs=(P(("dp", "vp"), None), P("dp")),
        check_vma=False,
    )
```

profile of v0, /device:TPU:1, one launch (start us, length us, event | category | flops | bytes accessed | tf_op | source)
XLA Modules:
  0.0 294.9 jit_solution(17968290493426970327)
XLA Ops:
  7.2 26.0 %fusion.10 = (f32[2048]{0:T(1024)S(1)}, f32[2048,256]{0,1:T(8,128)S(1)}) fusion(f32[2048]{0:T(1024)} %param.6, bf16[2048,12288]{1,0:T(8,128)(2,1)} %param.4, bf16[12288,256]{1,0:T(8,128)(2,1)} %param.5), kind=kOutput, calls=%fused_computation.29 | convolution fusion | flops 12885948416 | bytes 58736640 | tf_op jit(solution)/shard_map/dot_general | solution.py:13
  33.5 0.6 maximum_bitcast_fusion
  34.4 68.9 %all-gather.8.cloned.1.call-done = f32[128,2,2048]{2,1,0:T(2,128)} async-done(((f32[1,2,2048]{2,1,0:T(2,128)}), f32[128,2,2048]{2,1,0:T(2,128)}) %all-gather.8.cloned.1.call-update) | async-done | bytes 2097168 | tf_op jit(solution)/shard_map/all_gather | solution.py:18
  103.3 3.9 %slice_reduce_fusion = (f32[2048]{0:T(1024)S(1)}, f32[128,1,2048]{2,1,0:T(1,128)S(1)}, f32[128,1,2048]{2,1,0:T(1,128)S(1)}) fusion(f32[128,2,2048]{2,1,0:T(2,128)} %all-gather.8.cloned.1.call-done), kind=kLoop, calls=%fused_computation.28 | loop fusion | flops 260096 | bytes 4202496 | tf_op jit(solution)/shard_map/reduce_max | solution.py:19
  107.2 0.9 fusion.5
  108.4 1.6 fusion
  110.2 1.2 copy-done
  111.4 1.7 broadcast_add_fusion.2
  113.1 1.2 copy.20
  114.4 1.3 copy-done.1
  115.7 0.6 slice.27
  116.4 3.2 %copy.19 = f32[2048,2,128]{2,1,0:T(2,128)} copy(f32[2048,2,128]{0,1,2:T(2,128)S(1)} %bitcast.36) | data formatting | bytes 4194304 | tf_op jit(solution)/shard_map/reduce_window_sum
  119.5 2.9 reduce_window_sum.20
  122.5 55.1 %all-gather.6.cloned.1.call-done = f32[262144,1]{0,1:T(1,128)} async-done(((f32[2048,1]{0,1:T(1,128)}), f32[262144,1]{0,1:T(1,128)}) %all-gather.6.cloned.1.call-update) | async-done | bytes 1048592 | tf_op jit(solution)/shard_map/all_gather | solution.py:23
  177.5 0.5 broadcast.50
  178.0 10.6 %reduce.4 = f32[262144]{0:T(1024)S(1)} reduce(f32[262144,1]{0,1:T(1,128)} %all-gather.6.cloned.1.call-done, f32[]{:T(128)} %broadcast.50), dimensions={1}, to_apply=%all-gather.1.reduce_sub_computation.3 | reduce | bytes 2097156 | tf_op jit(solution)/shard_map/all_gather | solution.py:23
  188.6 1.1 reshape.76
  189.8 1.4 select_reduce_fusion
  191.2 1.7 broadcast_add_fusion.1
  192.9 5.8 %all-to-all-start = ((f32[128,16,256]{2,1,0:T(8,128)}), f32[128,16,256]{2,1,0:T(8,128)}, u32[]{:S(2)}, u32[]{:S(2)}) async-start(f32[128,16,256]{2,1,0:T(8,128)} %broadcast_add_fusion.1), calls=%async_computation | async-start | bytes 4194304 | tf_op jit(solution)/shard_map/all_to_all | solution.py:31
  198.8 1.8 broadcast_add_fusion
  200.7 16.8 %gather_fusion = f32[2048]{0:T(1024)S(1)} fusion(f32[2048,256]{0,1:T(8,128)S(1)} %broadcast_add_fusion, s32[2048]{0:T(1024)S(1)} %bitcast.34), kind=kCustom, calls=%fused_computation | custom fusion | bytes 32768 | tf_op jit(solution)/shard_map/jit(take_along_axis)/gather | solution.py:29
  217.5 67.5 %psum.7 = f32[2048]{0:T(1024)} all-reduce(f32[2048]{0:T(1024)S(1)} %select_select_fusion), channel_id=1, replica_groups=mesh['dp'=1,'vp'=128] {'vp'}, use_global_device_ids=true, to_apply=%region_7.8 | all-reduce | flops 2048 | bytes 16384 | tf_op jit(solution)/shard_map/psum | solution.py:30
  285.0 3.1 %copy.24 = f32[128,2,8,256]{3,2,0,1:T(8,128)} copy(f32[128,2,8,256]{3,2,1,0:T(8,128)} %bitcast.12) | data formatting | bytes 4194304 | tf_op jit(solution)/shard_map/all_to_all | solution.py:31
  (23 shorter events, 1.2 us)
Async XLA Ops:
  7.2 96.2 %all-gather.8.cloned.1.call-start = ((), (), s32[]{:S(2)}) async-start(), calls=%async_computation.2 | async-start | bytes 2113536 | tf_op jit(solution)/shard_map/all_gather | solution.py:18
  34.2 143.3 %all-gather.6.cloned.1.call-start = ((), (), s32[]{:S(2)}) async-start(), calls=%async_computation.1 | async-start | bytes 1056768 | tf_op jit(solution)/shard_map/all_gather | solution.py:23
  110.1 1.3 copy-start
  114.4 1.4 copy-start.1
  192.9 5.8 %copy-start.2 = (s32[2048]{0:T(1024)S(1)}, s32[2048]{0:T(1024)}, u32[]{:S(2)}) copy-start(s32[2048]{0:T(1024)} %param.7) | copy-start | bytes 24580
  192.9 92.1 %all-to-all-start = ((f32[128,16,256]{2,1,0:T(8,128)}), f32[128,16,256]{2,1,0:T(8,128)}, u32[]{:S(2)}, u32[]{:S(2)}) async-start(f32[128,16,256]{2,1,0:T(8,128)} %broadcast_add_fusion.1), calls=%async_computation | async-start | bytes 4194304 | tf_op jit(solution)/shard_map/all_to_all | solution.py:31
Sparse Core Ops, SparseCore 0:
  34.3 68.9 all-gather.7
  116.5 61.0 all-gather.5
where the time goes:
time: 296 us; the launch traced here: 295 us
  waiting for transfers between devices  124 us (42%)
  blocking collectives  67.5 us (23%)
  local copies, waits for them, and re-layouts  32.1 us (11%)
  matrix products  26 us (9%)
  other arithmetic  25 us (8%)
  between operations  14.2 us (5%)
  starting transfers between devices  6.09 us (2%)
    all_gather x1, waiting for transfers between devices, local_step(): shard_stats = lax.all_gather(jnp.stack([local_max, local_sum]), 'vp')  68.9 us
    psum x1, blocking collectives, local_step(): cdf_at_target = lax.psum(jnp.where(in_shard, picked, 0.0), 'vp')  67.5 us
    all_gather x1, waiting for transfers between devices, local_step(): totals = lax.all_gather(local_cdf[:, -1], 'vp')  55.1 us
    dot_general x1, matrix products, local_step(): logits = jnp.dot(hidden, w_local, preferred_element_type=jnp.float32)  26 us
    gather x1, local copies, waits for them, and re-layouts, local_step(): jnp.take_along_axis(cdf_cols, jnp.clip(local_ids, 0, local_vocab - 1)[:,...  16.8 us
    all_gather x1, other arithmetic, local_step(): totals = lax.all_gather(local_cdf[:, -1], 'vp')  10.6 us
    another operation x5, local copies, waits for them, and re-layouts  7.32 us
  transfers between devices with their start and end apart: 3, of which 2 were waited for; matrix products, arithmetic and copies ran while one was open for 8% of the time, Pallas kernels for 0%

commit v1 on v0

v1 whole, which is shorter than its diff:
```python
import functools

import jax
import jax.numpy as jnp
from jax import lax
from jax.experimental import pallas as pl
from jax.experimental.pallas import tpu as pltpu
from jax.sharding import PartitionSpec as P

MESH = pl.DeviceIdType.MESH
STRIDE = 37
SLOTS = 3


def split3(x):
    hi = x.astype(jnp.bfloat16)
    rest = x - hi.astype(jnp.float32)
    mid = rest.astype(jnp.bfloat16)
    lo = (rest - mid.astype(jnp.float32)).astype(jnp.bfloat16)
    return hi, mid, lo


def exact_dot(x, ones_mask):
    hi, mid, lo = split3(x)
    dot = functools.partial(jnp.dot, preferred_element_type=jnp.float32)
    return dot(lo, ones_mask) + dot(mid, ones_mask) + dot(hi, ones_mask)


def exchange_kernel(
    n, rows, group,
    hidden, w, temp, target,
    cum_out, scale_out, off_out, tgt_out,
    w_buf, h_buf, send, recv, cum, tsend, trecv,
    w_sem, h_sem, send_sem, recv_sem, out_sem, tsend_sem, trecv_sem,
):
    me = lax.axis_index("vp")
    cols = w.shape[1]
    steps = n // group
    bits = n.bit_length() - 1
    my_bits = [lax.rem(lax.div(me, 1 << i), 2) for i in range(bits)]

    def peer(k):
        p = lax.rem(k * STRIDE, n)
        return sum(lax.rem(my_bits[i] + lax.div(p, 1 << i), 2) * (1 << i) for i in range(bits))

    def h_copy(slot, j, d):
        return pltpu.make_async_copy(
            hidden.at[pl.ds(pl.multiple_of(d * rows, rows), rows)],
            h_buf.at[slot, pl.ds(j * rows, rows)],
            h_sem.at[slot],
        )

    def fetch(step):
        slot = lax.rem(step, SLOTS)
        for j in range(group):
            h_copy(slot, j, peer(step * group + j + 1)).start()

    def fetched(slot):
        pltpu.make_async_copy(h_buf.at[slot], h_buf.at[slot], h_sem.at[slot]).wait()

    w_parts = 4
    part = w.shape[0] // w_parts
    fetch(0)
    for i in range(w_parts):
        at = pl.ds(i * part, part)
        pltpu.make_async_copy(w.at[at], w_buf.at[at], w_sem).start()
    for s in range(1, SLOTS - 1):
        fetch(s)

    barrier = pltpu.get_barrier_semaphore()

    def greet(k, carry):
        pl.semaphore_signal(barrier, inc=1, device_id={"vp": peer(k)}, device_id_type=MESH)
        return carry

    lax.fori_loop(1, n, greet, 0)

    def block_copy(step, j):
        d = peer(step * group + j + 1)
        return pltpu.make_async_remote_copy(
            src_ref=send.at[step * group + j],
            dst_ref=recv.at[me],
            send_sem=send_sem,
            recv_sem=recv_sem.at[step],
            device_id={"vp": d},
            device_id_type=MESH,
        )

    def multiply(step):
        slot = lax.rem(step, SLOTS)
        z = jnp.dot(h_buf[slot], w_buf[...], preferred_element_type=jnp.float32)
        send[pl.ds(step * group, group)] = z.reshape(group, rows, cols)

    pltpu.make_async_copy(w_buf, w_buf, w_sem).wait()

    def matmul_step(step, carry):
        fetched(lax.rem(step, SLOTS))

        @pl.when(step == 1)
        def _():
            pl.semaphore_wait(barrier, n - 1)

        @pl.when(step >= 1)
        def _():
            for j in range(group):
                block_copy(step - 1, j).start()

        @pl.when(step + SLOTS - 1 < steps)
        def _():
            fetch(step + SLOTS - 1)

        multiply(step)
        return carry

    lax.fori_loop(0, steps, matmul_step, 0)

    per = 128 // rows
    lane = lax.broadcasted_iota(jnp.int32, (rows, 128), 1)
    row = lax.broadcasted_iota(jnp.int32, (rows, 128), 0)
    own_lane = lane == lax.rem(me, per) * rows + row
    own_at = pl.ds(lax.div(me, per), 1)
    t_col = jnp.sum(jnp.where(own_lane, temp[own_at, :], 0.0), axis=1, keepdims=True)
    g_col = jnp.sum(jnp.where(own_lane, target[own_at, :], 0), axis=1, keepdims=True)
    upto = (
        lax.broadcasted_iota(jnp.int32, (cols, cols), 0) <= lax.broadcasted_iota(jnp.int32, (cols, cols), 1)
    ).astype(jnp.float32).astype(jnp.bfloat16)
    col = lax.broadcasted_iota(jnp.int32, (rows, cols), 1)

    for j in range(group - 1):
        block_copy(steps - 1, j).start()
    recv[me] = send[n - 1]

    def take(step, carry):
        m_all, s_all, t_acc = carry

        @pl.when(step < steps - 1)
        def _():
            whole = recv.at[pl.ds(0, group)]
            pltpu.make_async_copy(whole, whole, recv_sem.at[step]).wait()

        @pl.when(step == steps - 1)
        def _():
            whole = recv.at[pl.ds(0, group - 1)]
            pltpu.make_async_copy(whole, whole, recv_sem.at[step]).wait()

        source = [peer(step * group + j + 1) for j in range(group)]
        z = [recv[s] * t_col for s in source]
        m = [jnp.max(v, axis=1, keepdims=True) for v in z]
        e = jnp.concatenate([jnp.exp(v - u) for v, u in zip(z, m)], axis=0)
        c = exact_dot(e, upto)
        for j, s in enumerate(source):
            c_j = c[j * rows : (j + 1) * rows]
            cum[s] = c_j
            here = lane == s
            m_all = jnp.where(here, m[j], m_all)
            s_all = jnp.where(here, c_j[:, cols - 1 :], s_all)
            t_acc = t_acc + jnp.where(col == g_col - s * cols, c_j, 0.0)
            pltpu.make_async_copy(cum.at[s], cum_out.at[s], out_sem).start()
        return m_all, s_all, t_acc

    zero = jnp.zeros((rows, 128), jnp.float32)
    m_all, s_all, t_acc = lax.fori_loop(0, steps, take, (zero, zero, jnp.zeros((rows, cols), jnp.float32)))

    top = jnp.max(m_all, axis=1, keepdims=True)
    weight = jnp.exp(m_all - top)
    mass = s_all * weight
    total = jnp.sum(mass, axis=1, keepdims=True)
    before = (
        lax.broadcasted_iota(jnp.int32, (n, n), 0) < lax.broadcasted_iota(jnp.int32, (n, n), 1)
    ).astype(jnp.float32).astype(jnp.bfloat16)
    scale = weight / total
    off = exact_dot(mass / total, before)
    t_cum = jnp.sum(t_acc, axis=1, keepdims=True)
    t_here = lane == lax.div(g_col, cols)
    t_scale = jnp.sum(jnp.where(t_here, scale, 0.0), axis=1, keepdims=True)
    t_off = jnp.sum(jnp.where(t_here, off, 0.0), axis=1, keepdims=True)
    t_val = t_cum * t_scale + t_off
    t_row = jnp.sum(jnp.where(own_lane, t_val, 0.0), axis=0, keepdims=True)
    tsend[...] = jnp.broadcast_to(t_row, tsend.shape)
    scale_out[...] = scale
    off_out[...] = off
    trecv[pl.ds(me, 1), :] = t_row
    pltpu.make_async_copy(cum, cum, out_sem).wait()

    def tell(k, carry):
        pltpu.make_async_remote_copy(
            src_ref=tsend.at[pl.ds(0, 1)],
            dst_ref=trecv.at[pl.ds(me, 1)],
            send_sem=tsend_sem,
            recv_sem=trecv_sem,
            device_id={"vp": peer(k)},
            device_id_type=MESH,
        ).start()
        return carry

    lax.fori_loop(1, n, tell, 0)
    others = trecv.at[pl.ds(0, n - 1)]
    pltpu.make_async_copy(others, others, trecv_sem).wait()
    tgt_out[...] = jnp.sum(trecv[...].reshape(n // per, per, 128), axis=1)
    pltpu.make_async_copy(others, others, tsend_sem).wait()
    sent = send.at[pl.ds(0, n - 1)]
    pltpu.make_async_copy(sent, sent, send_sem).wait()


def finish_kernel(span, cum, scale, off, tgt, table, tgt_out):
    shift = lax.rem(128 - pl.program_id(0) * span, 128)
    sc = pltpu.roll(scale[...], shift, 1)
    of = pltpu.roll(off[...], shift, 1)
    cols = cum.shape[2]
    for i in range(span):
        table[:, i * cols : (i + 1) * cols] = cum[i] * sc[:, i : i + 1] + of[:, i : i + 1]
    tgt_out[...] = tgt[...]


def solution(mesh):
    n = mesh.shape["vp"]

    def local_step(hidden, w_local, inv_temp, target_ids):
        batch, depth = hidden.shape
        cols = w_local.shape[1]
        rows = batch // n
        group = 8
        f32 = jnp.float32
        vmem = pl.BlockSpec(memory_space=pltpu.VMEM)
        hbm = pl.BlockSpec(memory_space=pl.ANY)
        cum, scale, off, tgt = pl.pallas_call(
            functools.partial(exchange_kernel, n, rows, group),
            out_shape=(
                jax.ShapeDtypeStruct((n, rows, cols), f32),
                jax.ShapeDtypeStruct((rows, 128), f32),
                jax.ShapeDtypeStruct((rows, 128), f32),
                jax.ShapeDtypeStruct((batch // 128, 128), f32),
            ),
            in_specs=[hbm, hbm, vmem, vmem],
            out_specs=(hbm, vmem, vmem, vmem),
            scratch_shapes=[
                pltpu.VMEM((depth, cols), jnp.bfloat16),
                pltpu.VMEM((SLOTS, group * rows, depth), jnp.bfloat16),
                pltpu.VMEM((n, rows, cols), f32),
                pltpu.VMEM((n, rows, cols), f32),
                pltpu.VMEM((n, rows, cols), f32),
                pltpu.VMEM((8, 128), f32),
                pltpu.VMEM((n, 128), f32),
                pltpu.SemaphoreType.DMA,
                pltpu.SemaphoreType.DMA((SLOTS,)),
                pltpu.SemaphoreType.DMA,
                pltpu.SemaphoreType.DMA((n // group,)),
                pltpu.SemaphoreType.DMA,
                pltpu.SemaphoreType.DMA,
                pltpu.SemaphoreType.DMA,
            ],
            compiler_params=pltpu.CompilerParams(
                collective_id=0, has_side_effects=True, vmem_limit_bytes=48 * 1024 * 1024
            ),
            name="exchange",
        )(hidden, w_local, inv_temp.reshape(-1, 128), target_ids.reshape(-1, 128))
        span = 16
        whole = lambda i: (0, 0)
        table, at_target = pl.pallas_call(
            functools.partial(finish_kernel, span),
            out_shape=(
                jax.ShapeDtypeStruct((rows, n * cols), f32),
                jax.ShapeDtypeStruct((batch // 128, 128), f32),
            ),
            grid=(n // span,),
            in_specs=[
                pl.BlockSpec((span, rows, cols), lambda i: (i, 0, 0)),
                pl.BlockSpec((rows, 128), whole),
                pl.BlockSpec((rows, 128), whole),
                pl.BlockSpec((batch // 128, 128), whole),
            ],
            out_specs=(
                pl.BlockSpec((rows, span * cols), lambda i: (0, i)),
                pl.BlockSpec((batch // 128, 128), whole),
            ),
            name="finish",
        )(cum, scale, off, tgt)
        return table, at_target.reshape(-1)

    return jax.shard_map(
        local_step,
        mesh=mesh,
        in_specs=(P("dp", None), P(None, "vp"), P("dp"), P("dp")),
        out_specs=(P(("dp", "vp"), None), P("dp")),
        check_vma=False,
    )
```

time: 296 us -> 77.9 us (0.26)
  waiting for transfers between devices: 124 us -> 0 us
  Pallas kernels: 0 us -> 72.4 us
  blocking collectives: 67.5 us -> 0 us
  local copies, waits for them, and re-layouts: 32.1 us -> 4.51 us
  matrix products: 26 us -> 0 us
  other arithmetic: 25 us -> 0 us
  between operations: 14.2 us -> 0.66 us
  starting transfers between devices: 6.09 us -> 0 us
    all_gather x2 -> x0, waiting for transfers between devices: 124 us -> none  [the longest x1 68.9 us: local_step(): shard_stats = lax.all_gather(jnp.stack([local_max, local_sum]), 'vp')]
    pallas_call x0 -> x2, Pallas kernels: none -> 72.4 us  [the longest x1 66 us: local_step(): pl.pallas_call(functools.partial(exchange_kernel, n, rows, group), out_sh...]
    psum x1 -> x0, blocking collectives: 67.5 us -> none  [local_step(): cdf_at_target = lax.psum(jnp.where(in_shard, picked, 0.0), 'vp')]
    dot_general x1 -> x0, matrix products: 26 us -> none  [local_step(): logits = jnp.dot(hidden, w_local, preferred_element_type=jnp.float32)]
    gather x1 -> x0, local copies, waits for them, and re-layouts: 16.8 us -> none  [local_step(): jnp.take_along_axis(cdf_cols, jnp.clip(local_ids, 0, local_vocab - 1)[:,...]
    all_gather x1 -> x0, other arithmetic: 10.6 us -> none  [local_step(): totals = lax.all_gather(local_cdf[:, -1], 'vp')]
    another operation x5 -> x0, local copies, waits for them, and re-layouts: 7.32 us -> none
    all_to_all x1 -> x0, starting transfers between devices: 5.83 us -> none  [local_step(): cdf_rows = lax.all_to_all(cdf_cols, 'vp', 0, 1, tiled=True)]
  transfers between devices with their start and end apart: 3 -> 0, of which waited for: 2 -> 0; matrix products, arithmetic and copies ran while one was open for 8% -> 0% of each run, Pallas kernels for 0% -> 0%
where the time goes in v1:
time: 77.9 us; the launch traced here: 77.6 us
  Pallas kernels  72.4 us (93%)
  local copies, waits for them, and re-layouts  4.51 us (6%)
    pallas_call x1, Pallas kernels, local_step(): pl.pallas_call(functools.partial(exchange_kernel, n, rows, group), out_sh...  66 us
    pallas_call x1, Pallas kernels, local_step(): pl.pallas_call(functools.partial(finish_kernel, span), out_shape=(jax.Sha...  6.42 us
    unnamed x12, local copies, waits for them, and re-layouts  4.51 us

profile of v1, /device:TPU:1, one launch (start us, length us, event | category | flops | bytes accessed | tf_op | source)
XLA Modules:
  0.0 77.6 jit_solution(13179619876643564366)
XLA Ops:
  0.6 0.0 copy-start.1
  0.6 0.7 copy-done.1
  1.3 0.0 copy-start.2
  1.3 0.7 copy-done.2
  2.0 66.0 %exchange.1 = (f32[128,16,256]{2,1,0:T(8,128)S(1)}, f32[16,128]{1,0:T(8,128)S(1)}, f32[16,128]{1,0:T(8,128)S(1)}, f32[16,128]{1,0:T(8,128)S(1)}) custom-call(bf16[2048,12288]{1,0:T(8,128)(2,1)} %hidden.1, bf16[12288,256]{1,0:T(8,128)(2,1)} %w.1, f32[16,128]{1,0:T(8,128)S(1)} %bitcast.3, s32[16,128]{1,0:T(8,128)S(1)} %bitcast.4), custom_call_target="tpu_custom_call" | custom-call | tf_op jit(solution)/shard_map/exchange/pallas_call | solution.py:226
  68.0 0.0 copy-start
  68.0 1.3 %copy-done = f32[128,16,256]{2,1,0:T(8,128)} copy-done((f32[128,16,256]{2,1,0:T(8,128)}, f32[128,16,256]{2,1,0:T(8,128)S(1)}, u32[]{:S(2)}) %copy-start) | copy-done | bytes 2097176
  69.4 0.0 copy-start.3
  69.4 0.6 copy-done.3
  70.0 0.0 copy-start.4
  70.0 0.6 copy-done.4
  70.6 0.0 copy-start.5
  70.6 0.6 copy-done.5
  71.2 6.4 %finish.1 = (f32[16,32768]{1,0:T(8,128)}, f32[16,128]{1,0:T(8,128)}) custom-call(f32[128,16,256]{2,1,0:T(8,128)} %copy-done, f32[16,128]{1,0:T(8,128)} %copy-done.3, f32[16,128]{1,0:T(8,128)} %copy-done.4, f32[16,128]{1,0:T(8,128)} %copy-done.5), custom_call_target="tpu_custom_call" | custom-call | tf_op jit(solution)/shard_map/finish/pallas_call | solution.py:259
Async XLA Ops:
  0.6 0.7 copy-start.1
  1.3 0.7 copy-start.2
  68.0 1.3 %copy-start = (f32[128,16,256]{2,1,0:T(8,128)}, f32[128,16,256]{2,1,0:T(8,128)S(1)}, u32[]{:S(2)}) copy-start(f32[128,16,256]{2,1,0:T(8,128)S(1)} %get-tuple-element.8.cum) | copy-start | bytes 6291460
  69.4 0.6 copy-start.3
  70.0 0.6 copy-start.4
  70.6 0.6 copy-start.5

commit v2 on v1

v2 whole, which is shorter than its diff:
```python
import functools

import jax
import jax.numpy as jnp
from jax import lax
from jax.experimental import pallas as pl
from jax.experimental.pallas import tpu as pltpu
from jax.sharding import PartitionSpec as P

MESH = pl.DeviceIdType.MESH
SLOTS = 3
FINE = ((1, 3, 5), (2, 4, 6), (0,))
COARSE = (3, 4, 5, 6)


def split3(x):
    hi = x.astype(jnp.bfloat16)
    rest = x - hi.astype(jnp.float32)
    mid = rest.astype(jnp.bfloat16)
    lo = (rest - mid.astype(jnp.float32)).astype(jnp.bfloat16)
    return hi, mid, lo


def exact_dot(x, ones_mask):
    hi, mid, lo = split3(x)
    dot = functools.partial(jnp.dot, preferred_element_type=jnp.float32)
    return dot(lo, ones_mask) + dot(mid, ones_mask) + dot(hi, ones_mask)


def partners(me, step, steps):
    turned = steps - 1 - step
    bits = []
    for i in range(7):
        bit = lax.rem(lax.div(me, 1 << i), 2)
        if i in COARSE:
            bit = lax.rem(bit + lax.div(turned, 1 << COARSE.index(i)), 2)
        bits.append(bit)
    base = sum(b * (1 << i) for i, b in enumerate(bits))
    move = [sum((1 - 2 * bits[i]) * (1 << i) for i in fine) for fine in FINE]
    return [base + sum(m for t, m in enumerate(move) if (7 - j) >> t & 1) for j in range(8)]


def exchange_kernel(
    n, rows, group,
    hidden, w, temp_hbm, target_hbm,
    table, tgt_out,
    w_buf, h_buf, send, recv, cum, temp, target, tsend, trecv,
    w_sem, h_sem, send_sem, recv_sem, small_sem, tsend_sem, trecv_sem,
):
    me = lax.axis_index("vp")
    cols = w.shape[1]
    steps = n // group

    def fetch(step):
        slot = lax.rem(step, SLOTS)
        for j, d in enumerate(partners(me, step, steps)):
            pltpu.make_async_copy(
                hidden.at[pl.ds(pl.multiple_of(d * rows, rows), rows)],
                h_buf.at[slot, pl.ds(j * rows, rows)],
                h_sem.at[slot],
            ).start()

    fetch(0)
    part = w.shape[0] // 4
    for i in range(4):
        at = pl.ds(i * part, part)
        pltpu.make_async_copy(w.at[at], w_buf.at[at], w_sem).start()
    barrier = pltpu.get_barrier_semaphore()

    def greet(step, carry):
        for j, d in enumerate(partners(me, step, steps)):
            if j < group - 1:
                pl.semaphore_signal(barrier, inc=1, device_id={"vp": d}, device_id_type=MESH)
            else:

                @pl.when(step < steps - 1)
                def _():
                    pl.semaphore_signal(barrier, inc=1, device_id={"vp": d}, device_id_type=MESH)

        return carry

    lax.fori_loop(0, steps, greet, 0)
    for s in range(1, SLOTS - 1):
        fetch(s)
    pltpu.make_async_copy(temp_hbm, temp, small_sem).start()
    pltpu.make_async_copy(target_hbm, target, small_sem).start()

    def send_blocks(step, count):
        for j, d in enumerate(partners(me, step, steps)[:count]):
            pltpu.make_async_remote_copy(
                src_ref=send.at[step * group + j],
                dst_ref=recv.at[me],
                send_sem=send_sem,
                recv_sem=recv_sem.at[step],
                device_id={"vp": d},
                device_id_type=MESH,
            ).start()

    pltpu.make_async_copy(w_buf, w_buf, w_sem).wait()

    def matmul_step(step, carry):
        slot = lax.rem(step, SLOTS)
        pltpu.make_async_copy(h_buf.at[slot], h_buf.at[slot], h_sem.at[slot]).wait()

        @pl.when(step == 1)
        def _():
            pl.semaphore_wait(barrier, n - 1)

        @pl.when(step >= 1)
        def _():
            send_blocks(step - 1, group)

        @pl.when(step + SLOTS - 1 < steps)
        def _():
            fetch(step + SLOTS - 1)

        z = jnp.dot(h_buf[slot], w_buf[...], preferred_element_type=jnp.float32)
        send[pl.ds(step * group, group)] = z.reshape(group, rows, cols)
        return carry

    lax.fori_loop(0, steps, matmul_step, 0)
    pltpu.make_async_copy(temp, temp, small_sem).wait()
    pltpu.make_async_copy(target, target, small_sem).wait()

    per = 128 // rows
    lane = lax.broadcasted_iota(jnp.int32, (rows, 128), 1)
    row = lax.broadcasted_iota(jnp.int32, (rows, 128), 0)
    own_lane = lane == lax.rem(me, per) * rows + row
    own_at = pl.ds(lax.div(me, per), 1)
    t_col = jnp.sum(jnp.where(own_lane, temp[own_at, :], 0.0), axis=1, keepdims=True)
    g_col = jnp.sum(jnp.where(own_lane, target[own_at, :], 0), axis=1, keepdims=True)
    upto = (
        lax.broadcasted_iota(jnp.int32, (cols, cols), 0) <= lax.broadcasted_iota(jnp.int32, (cols, cols), 1)
    ).astype(jnp.float32).astype(jnp.bfloat16)
    col = lax.broadcasted_iota(jnp.int32, (rows, cols), 1)

    send_blocks(steps - 1, group - 1)
    recv[me] = send[n - 1]

    def take(step, carry):
        m_all, s_all, t_acc = carry

        @pl.when(step < steps - 1)
        def _():
            whole = recv.at[pl.ds(0, group)]
            pltpu.make_async_copy(whole, whole, recv_sem.at[step]).wait()

        @pl.when(step == steps - 1)
        def _():
            whole = recv.at[pl.ds(0, group - 1)]
            pltpu.make_async_copy(whole, whole, recv_sem.at[step]).wait()

        source = partners(me, step, steps)
        z = [recv[s] * t_col for s in source]
        m = [jnp.max(v, axis=1, keepdims=True) for v in z]
        e = jnp.concatenate([jnp.exp(v - u) for v, u in zip(z, m)], axis=0)
        c = exact_dot(e, upto)
        for j, s in enumerate(source):
            c_j = c[j * rows : (j + 1) * rows]
            cum[s] = c_j
            here = lane == s
            m_all = jnp.where(here, m[j], m_all)
            s_all = jnp.where(here, c_j[:, cols - 1 :], s_all)
            t_acc = t_acc + jnp.where(col == g_col - s * cols, c_j, 0.0)
        return m_all, s_all, t_acc

    zero = jnp.zeros((rows, 128), jnp.float32)
    m_all, s_all, t_acc = lax.fori_loop(0, steps, take, (zero, zero, jnp.zeros((rows, cols), jnp.float32)))

    top = jnp.max(m_all, axis=1, keepdims=True)
    weight = jnp.exp(m_all - top)
    mass = s_all * weight
    total = jnp.sum(mass, axis=1, keepdims=True)
    before = (
        lax.broadcasted_iota(jnp.int32, (n, n), 0) < lax.broadcasted_iota(jnp.int32, (n, n), 1)
    ).astype(jnp.float32).astype(jnp.bfloat16)
    scale = weight / total
    off = exact_dot(mass / total, before)
    t_cum = jnp.sum(t_acc, axis=1, keepdims=True)
    t_here = lane == lax.div(g_col, cols)
    t_scale = jnp.sum(jnp.where(t_here, scale, 0.0), axis=1, keepdims=True)
    t_off = jnp.sum(jnp.where(t_here, off, 0.0), axis=1, keepdims=True)
    t_val = t_cum * t_scale + t_off
    t_row = jnp.sum(jnp.where(own_lane, t_val, 0.0), axis=0, keepdims=True)
    tsend[...] = jnp.broadcast_to(t_row, tsend.shape)
    trecv[pl.ds(me, 1), :] = t_row
    sent = send.at[pl.ds(0, n - 1)]
    pltpu.make_async_copy(sent, sent, send_sem).wait()

    def tell_one(d):
        pltpu.make_async_remote_copy(
            src_ref=tsend.at[pl.ds(0, 1)],
            dst_ref=trecv.at[pl.ds(me, 1)],
            send_sem=tsend_sem,
            recv_sem=trecv_sem,
            device_id={"vp": d},
            device_id_type=MESH,
        ).start()

    def tell(step, carry):
        for j, d in enumerate(partners(me, step, steps)):
            if j < group - 1:
                tell_one(d)
            else:
                pl.when(step < steps - 1)(functools.partial(tell_one, d))
        return carry

    lax.fori_loop(0, steps, tell, 0)
    for s in range(n):
        table[:, s * cols : (s + 1) * cols] = cum[s] * scale[:, s : s + 1] + off[:, s : s + 1]
    others = trecv.at[pl.ds(0, n - 1)]
    pltpu.make_async_copy(others, others, trecv_sem).wait()
    tgt_out[...] = jnp.sum(trecv[...].reshape(n // per, per, 128), axis=1)
    pltpu.make_async_copy(others, others, tsend_sem).wait()


def solution(mesh):
    n = mesh.shape["vp"]

    def local_step(hidden, w_local, inv_temp, target_ids):
        batch, depth = hidden.shape
        cols = w_local.shape[1]
        rows = batch // n
        group = 8
        f32 = jnp.float32
        vmem = pl.BlockSpec(memory_space=pltpu.VMEM)
        hbm = pl.BlockSpec(memory_space=pltpu.HBM)
        small = (batch // 128, 128)
        table, at_target = pl.pallas_call(
            functools.partial(exchange_kernel, n, rows, group),
            out_shape=(
                jax.ShapeDtypeStruct((rows, n * cols), f32),
                jax.ShapeDtypeStruct(small, f32),
            ),
            in_specs=[hbm] * 4,
            out_specs=(vmem, vmem),
            scratch_shapes=[
                pltpu.VMEM((depth, cols), jnp.bfloat16),
                pltpu.VMEM((SLOTS, group * rows, depth), jnp.bfloat16),
                pltpu.VMEM((n, rows, cols), f32),
                pltpu.VMEM((n, rows, cols), f32),
                pltpu.VMEM((n, rows, cols), f32),
                pltpu.VMEM(small, f32),
                pltpu.VMEM(small, jnp.int32),
                pltpu.VMEM((8, 128), f32),
                pltpu.VMEM((n, 128), f32),
                pltpu.SemaphoreType.DMA,
                pltpu.SemaphoreType.DMA((SLOTS,)),
                pltpu.SemaphoreType.DMA,
                pltpu.SemaphoreType.DMA((n // group,)),
                pltpu.SemaphoreType.DMA,
                pltpu.SemaphoreType.DMA,
                pltpu.SemaphoreType.DMA,
            ],
            compiler_params=pltpu.CompilerParams(
                collective_id=0, has_side_effects=True, vmem_limit_bytes=48 * 1024 * 1024
            ),
            name="exchange",
        )(hidden, w_local, inv_temp.reshape(small), target_ids.reshape(small))
        return table, at_target.reshape(-1)

    return jax.shard_map(
        local_step,
        mesh=mesh,
        in_specs=(P("dp", None), P(None, "vp"), P("dp"), P("dp")),
        out_specs=(P(("dp", "vp"), None), P("dp")),
        check_vma=False,
    )
```

time: 77.9 us -> 56.8 us (0.73)
  Pallas kernels: 72.4 us -> 52.6 us
  local copies, waits for them, and re-layouts: 4.51 us -> 3.31 us
    pallas_call x1, Pallas kernels: 66 us -> 52.6 us  [local_step(): pl.pallas_call(functools.partial(exchange_kernel, n, rows, group), out_sh...]
    pallas_call x1 -> x0, Pallas kernels: 6.42 us -> none  [local_step(): pl.pallas_call(functools.partial(finish_kernel, span), out_shape=(jax.Sha...]
    unnamed x12 -> x6, local copies, waits for them, and re-layouts: 4.51 us -> 3.31 us
where the time goes in v2:
time: 56.8 us; the launch traced here: 56.6 us
  Pallas kernels  52.6 us (93%)
  local copies, waits for them, and re-layouts  3.31 us (6%)
  between operations  0.65 us (1%)
    pallas_call x1, Pallas kernels, local_step(): pl.pallas_call(functools.partial(exchange_kernel, n, rows, group), out_sh...  52.6 us
    unnamed x6, local copies, waits for them, and re-layouts  3.31 us

profile of v2, /device:TPU:1, one launch (start us, length us, event | category | flops | bytes accessed | tf_op | source)
XLA Modules:
  0.0 56.6 jit_solution(11391593527577943910)
XLA Ops:
  0.6 0.0 copy-start
  0.6 0.7 %copy-done = f32[2048]{0:T(1024)S(1)} copy-done((f32[2048]{0:T(1024)S(1)}, f32[2048]{0:T(1024)}, u32[]{:S(2)}) %copy-start) | copy-done | bytes 8216
  1.3 0.0 copy-start.1
  1.3 0.7 %copy-done.1 = s32[2048]{0:T(1024)S(1)} copy-done((s32[2048]{0:T(1024)S(1)}, s32[2048]{0:T(1024)}, u32[]{:S(2)}) %copy-start.1) | copy-done | bytes 8216
  2.0 52.6 %exchange.1 = (f32[16,32768]{1,0:T(8,128)S(1)}, f32[16,128]{1,0:T(8,128)S(1)}) custom-call(bf16[2048,12288]{1,0:T(8,128)(2,1)} %hidden.1, bf16[12288,256]{1,0:T(8,128)(2,1)} %w.1, f32[16,128]{1,0:T(8,128)S(1)} %bitcast.3, s32[16,128]{1,0:T(8,128)S(1)} %bitcast.4), custom_call_target="tpu_custom_call" | custom-call | tf_op jit(solution)/shard_map/exchange/pallas_call | solution.py:229
  54.7 1.3 %copy.8 = f32[16,32768]{1,0:T(8,128)} copy(f32[16,32768]{1,0:T(8,128)S(1)} %get-tuple-element.8) | data formatting | bytes 4194304
  56.0 0.6 %copy.9 = f32[2048]{0:T(1024)} copy(f32[2048]{0:T(1024)S(1)} %bitcast.5) | data formatting | bytes 16384
Async XLA Ops:
  0.6 0.7 %copy-start = (f32[2048]{0:T(1024)S(1)}, f32[2048]{0:T(1024)}, u32[]{:S(2)}) copy-start(f32[2048]{0:T(1024)} %param.6) | copy-start | bytes 24580
  1.3 0.7 %copy-start.1 = (s32[2048]{0:T(1024)S(1)}, s32[2048]{0:T(1024)}, u32[]{:S(2)}) copy-start(s32[2048]{0:T(1024)} %param.7) | copy-start | bytes 24580

commit v3 on v2

--- a/solution.py
+++ b/solution.py
@@ -9,8 +9,9 @@
 
 MESH = pl.DeviceIdType.MESH
 SLOTS = 3
-FINE = ((1, 3, 5), (2, 4, 6), (0,))
-COARSE = (3, 4, 5, 6)
+FINE = ((1, 4, 6), (3, 6, 2), (5, 2, 4))
+COARSE = (0, 2, 4, 6)
+PACE = (1, 1)
 
 
 def split3(x):
@@ -27,17 +28,28 @@
     return dot(lo, ones_mask) + dot(mid, ones_mask) + dot(hi, ones_mask)
 
 
-def partners(me, step, steps):
+def partners(me, step, steps, sign=1):
     turned = steps - 1 - step
-    bits = []
-    for i in range(7):
-        bit = lax.rem(lax.div(me, 1 << i), 2)
-        if i in COARSE:
-            bit = lax.rem(bit + lax.div(turned, 1 << COARSE.index(i)), 2)
-        bits.append(bit)
-    base = sum(b * (1 << i) for i, b in enumerate(bits))
-    move = [sum((1 - 2 * bits[i]) * (1 << i) for i in fine) for fine in FINE]
-    return [base + sum(m for t, m in enumerate(move) if (7 - j) >> t & 1) for j in range(8)]
+    coarse = [lax.rem(lax.div(turned, 1 << COARSE.index(i)), 2) if i in COARSE else 0 for i in range(7)]
+    flipped = lambda bit, flip: 1 - bit if flip else bit
+    core = lax.rem(me, 2)
+    own = [lax.rem(lax.div(me, 2 * 4**a), 4) for a in range(3)]
+    known = {}
+    group = []
+    for j in range(8):
+        fine = [sum(i in f for t, f in enumerate(FINE) if (7 - j) >> t & 1) % 2 for i in range(7)]
+        if (0, fine[0]) not in known:
+            known[0, fine[0]] = lax.rem(core + flipped(coarse[0], fine[0]), 2)
+        parts = [known[0, fine[0]]]
+        for a in range(3):
+            low, high = fine[2 * a + 1], fine[2 * a + 2]
+            if (a + 1, low, high) not in known:
+                offset = flipped(coarse[2 * a + 1], low) + 2 * flipped(coarse[2 * a + 2], high)
+                moved = own[a] + offset if sign > 0 else own[a] + 4 - offset
+                known[a + 1, low, high] = lax.rem(moved, 4) * (2 * 4**a)
+            parts.append(known[a + 1, low, high])
+        group.append(sum(parts))
+    return group
 
 
 def exchange_kernel(
@@ -60,26 +72,26 @@
                 h_sem.at[slot],
             ).start()
 
+    barrier = pltpu.get_barrier_semaphore()
+
+    def greet(step, carry):
+        for j, d in enumerate(partners(me, step, steps)):
+            if j < group - 1:
+                pl.semaphore_signal(barrier, inc=1, device_id={"vp": d}, device_id_type=MESH)
+            else:
+
+                @pl.when(step < steps - 1)
+                def _():
+                    pl.semaphore_signal(barrier, inc=1, device_id={"vp": d}, device_id_type=MESH)
+
+        return carry
+
+    lax.fori_loop(0, steps, greet, 0)
     fetch(0)
     part = w.shape[0] // 4
     for i in range(4):
         at = pl.ds(i * part, part)
         pltpu.make_async_copy(w.at[at], w_buf.at[at], w_sem).start()
-    barrier = pltpu.get_barrier_semaphore()
-
-    def greet(step, carry):
-        for j, d in enumerate(partners(me, step, steps)):
-            if j < group - 1:
-                pl.semaphore_signal(barrier, inc=1, device_id={"vp": d}, device_id_type=MESH)
-            else:
-
-                @pl.when(step < steps - 1)
-                def _():
-                    pl.semaphore_signal(barrier, inc=1, device_id={"vp": d}, device_id_type=MESH)
-
-        return carry
-
-    lax.fori_loop(0, steps, greet, 0)
     for s in range(1, SLOTS - 1):
         fetch(s)
     pltpu.make_async_copy(temp_hbm, temp, small_sem).start()
@@ -98,6 +110,9 @@
 
     pltpu.make_async_copy(w_buf, w_buf, w_sem).wait()
 
+    def due(step):
+        return lax.div(jnp.maximum(step, 0) * PACE[0], PACE[1])
+
     def matmul_step(step, carry):
         slot = lax.rem(step, SLOTS)
         pltpu.make_async_copy(h_buf.at[slot], h_buf.at[slot], h_sem.at[slot]).wait()
@@ -106,9 +121,9 @@
         def _():
             pl.semaphore_wait(barrier, n - 1)
 
-        @pl.when(step >= 1)
-        def _():
-            send_blocks(step - 1, group)
+        @pl.when(due(step) > due(step - 1))
+        def _():
+            send_blocks(due(step) - 1, group)
 
         @pl.when(step + SLOTS - 1 < steps)
         def _():
@@ -134,7 +149,8 @@
     ).astype(jnp.float32).astype(jnp.bfloat16)
     col = lax.broadcasted_iota(jnp.int32, (rows, cols), 1)
 
-    send_blocks(steps - 1, group - 1)
+    for step in range((steps - 1) * PACE[0] // PACE[1], steps):
+        send_blocks(step, group if step < steps - 1 else group - 1)
     recv[me] = send[n - 1]
 
     def take(step, carry):
@@ -150,7 +166,7 @@
             whole = recv.at[pl.ds(0, group - 1)]
             pltpu.make_async_copy(whole, whole, recv_sem.at[step]).wait()
 
-        source = partners(me, step, steps)
+        source = partners(me, step, steps, -1)
         z = [recv[s] * t_col for s in source]
         m = [jnp.max(v, axis=1, keepdims=True) for v in z]
         e = jnp.concatenate([jnp.exp(v - u) for v, u in zip(z, m)], axis=0)
@@ -212,6 +228,19 @@
     pltpu.make_async_copy(others, others, trecv_sem).wait()
     tgt_out[...] = jnp.sum(trecv[...].reshape(n // per, per, 128), axis=1)
     pltpu.make_async_copy(others, others, tsend_sem).wait()
+
+
+def store_kernel(parts, table, tgt, table_out, tgt_out, sem):
+    cols = table.shape[1] // parts
+    copies = [
+        pltpu.make_async_copy(table.at[:, pl.ds(i * cols, cols)], table_out.at[:, pl.ds(i * cols, cols)], sem.at[i])
+        for i in range(parts)
+    ]
+    copies.append(pltpu.make_async_copy(tgt, tgt_out, sem.at[parts]))
+    for copy in copies:
+        copy.start()
+    for copy in copies:
+        copy.wait()
 
 
 def solution(mesh):
@@ -256,7 +285,22 @@
                 collective_id=0, has_side_effects=True, vmem_limit_bytes=48 * 1024 * 1024
             ),
             name="exchange",
-        )(hidden, w_local, inv_temp.reshape(small), target_ids.reshape(small))
+        )(
+            hidden,
+            w_local,
+            pltpu.with_memory_space_constraint(inv_temp.reshape(small), pltpu.HBM),
+            pltpu.with_memory_space_constraint(target_ids.reshape(small), pltpu.HBM),
+        )
+        parts = 4
+        table, at_target = pl.pallas_call(
+            functools.partial(store_kernel, parts),
+            out_shape=(jax.ShapeDtypeStruct(table.shape, f32), jax.ShapeDtypeStruct(small, f32)),
+            in_specs=[hbm] * 2,
+            out_specs=(hbm, hbm),
+            scratch_shapes=[pltpu.SemaphoreType.DMA((parts + 1,))],
+            compiler_params=pltpu.CompilerParams(vmem_limit_bytes=1024 * 1024),
+            name="store",
+        )(table, at_target)
         return table, at_target.reshape(-1)
 
     return jax.shard_map(

time: 56.8 us -> 54.7 us (0.963)
  local copies, waits for them, and re-layouts: 3.31 us -> 0 us
  Pallas kernels: 52.6 us -> 53.9 us
    unnamed x6 -> x0, local copies, waits for them, and re-layouts: 3.31 us -> none
    pallas_call x0 -> x1, Pallas kernels: none -> 1.36 us  [local_step(): pl.pallas_call(functools.partial(store_kernel, parts), out_shape=(jax.Sha...]
where the time goes in v3:
time: 54.7 us; the launch traced here: 54.6 us
  Pallas kernels  53.9 us (99%)
  between operations  0.64 us (1%)
    pallas_call x1, Pallas kernels, local_step(): pl.pallas_call(functools.partial(exchange_kernel, n, rows, group), out_sh...  52.6 us
    pallas_call x1, Pallas kernels, local_step(): pl.pallas_call(functools.partial(store_kernel, parts), out_shape=(jax.Sha...  1.36 us

profile of v3, /device:TPU:1, one launch (start us, length us, event | category | flops | bytes accessed | tf_op | source)
XLA Modules:
  0.0 54.6 jit_solution(5877431465698803308)
XLA Ops:
  0.6 52.6 %exchange.1 = (f32[16,32768]{1,0:T(8,128)S(1)}, f32[16,128]{1,0:T(8,128)S(1)}) custom-call(bf16[2048,12288]{1,0:T(8,128)(2,1)} %hidden.1, bf16[12288,256]{1,0:T(8,128)(2,1)} %w.1, f32[16,128]{1,0:T(8,128)} %bitcast.3, s32[16,128]{1,0:T(8,128)} %bitcast.4), custom_call_target="tpu_custom_call" | custom-call | tf_op jit(solution)/shard_map/exchange/pallas_call | solution.py:258
  53.2 1.4 %store.1 = (f32[16,32768]{1,0:T(8,128)}, f32[16,128]{1,0:T(8,128)}) custom-call(f32[16,32768]{1,0:T(8,128)S(1)} %get-tuple-element.6.table, f32[16,128]{1,0:T(8,128)S(1)} %get-tuple-element.7.tgt), custom_call_target="tpu_custom_call" | custom-call | tf_op jit(solution)/shard_map/store/pallas_call | solution.py:295

commit v4 on v3

--- a/solution.py
+++ b/solution.py
@@ -9,8 +9,9 @@
 
 MESH = pl.DeviceIdType.MESH
 SLOTS = 3
-FINE = ((1, 4, 6), (3, 6, 2), (5, 2, 4))
+FINE = ((1, 4), (3, 6), (5, 2))
 COARSE = (0, 2, 4, 6)
+TAKE = 2
 PACE = (1, 1)
 
 
@@ -153,20 +154,18 @@
         send_blocks(step, group if step < steps - 1 else group - 1)
     recv[me] = send[n - 1]
 
-    def take(step, carry):
+    def arrived(step, count):
+        whole = recv.at[pl.ds(0, count)]
+        pltpu.make_async_copy(whole, whole, recv_sem.at[step]).wait()
+
+    def take(turn, carry):
         m_all, s_all, t_acc = carry
-
-        @pl.when(step < steps - 1)
-        def _():
-            whole = recv.at[pl.ds(0, group)]
-            pltpu.make_async_copy(whole, whole, recv_sem.at[step]).wait()
-
-        @pl.when(step == steps - 1)
-        def _():
-            whole = recv.at[pl.ds(0, group - 1)]
-            pltpu.make_async_copy(whole, whole, recv_sem.at[step]).wait()
-
-        source = partners(me, step, steps, -1)
+        first = turn * TAKE
+        for i in range(TAKE - 1):
+            arrived(first + i, group)
+        pl.when(turn < steps // TAKE - 1)(functools.partial(arrived, first + TAKE - 1, group))
+        pl.when(turn == steps // TAKE - 1)(functools.partial(arrived, first + TAKE - 1, group - 1))
+        source = [d for i in range(TAKE) for d in partners(me, first + i, steps, -1)]
         z = [recv[s] * t_col for s in source]
         m = [jnp.max(v, axis=1, keepdims=True) for v in z]
         e = jnp.concatenate([jnp.exp(v - u) for v, u in zip(z, m)], axis=0)
@@ -181,21 +180,18 @@
         return m_all, s_all, t_acc
 
     zero = jnp.zeros((rows, 128), jnp.float32)
-    m_all, s_all, t_acc = lax.fori_loop(0, steps, take, (zero, zero, jnp.zeros((rows, cols), jnp.float32)))
+    m_all, s_all, t_acc = lax.fori_loop(0, steps // TAKE, take, (zero, zero, jnp.zeros((rows, cols), jnp.float32)))
 
     top = jnp.max(m_all, axis=1, keepdims=True)
     weight = jnp.exp(m_all - top)
     mass = s_all * weight
     total = jnp.sum(mass, axis=1, keepdims=True)
-    before = (
-        lax.broadcasted_iota(jnp.int32, (n, n), 0) < lax.broadcasted_iota(jnp.int32, (n, n), 1)
-    ).astype(jnp.float32).astype(jnp.bfloat16)
     scale = weight / total
-    off = exact_dot(mass / total, before)
+    share = mass / total
     t_cum = jnp.sum(t_acc, axis=1, keepdims=True)
     t_here = lane == lax.div(g_col, cols)
     t_scale = jnp.sum(jnp.where(t_here, scale, 0.0), axis=1, keepdims=True)
-    t_off = jnp.sum(jnp.where(t_here, off, 0.0), axis=1, keepdims=True)
+    t_off = jnp.sum(jnp.where(lane < lax.div(g_col, cols), share, 0.0), axis=1, keepdims=True)
     t_val = t_cum * t_scale + t_off
     t_row = jnp.sum(jnp.where(own_lane, t_val, 0.0), axis=0, keepdims=True)
     tsend[...] = jnp.broadcast_to(t_row, tsend.shape)
@@ -222,6 +218,10 @@
         return carry
 
     lax.fori_loop(0, steps, tell, 0)
+    before = (
+        lax.broadcasted_iota(jnp.int32, (n, n), 0) < lax.broadcasted_iota(jnp.int32, (n, n), 1)
+    ).astype(jnp.float32).astype(jnp.bfloat16)
+    off = exact_dot(share, before)
     for s in range(n):
         table[:, s * cols : (s + 1) * cols] = cum[s] * scale[:, s : s + 1] + off[:, s : s + 1]
     others = trecv.at[pl.ds(0, n - 1)]

time: 54.7 us -> 51.7 us (0.945)
  Pallas kernels: 53.9 us -> 50.9 us
    pallas_call x1, Pallas kernels: 52.6 us -> 49.6 us  [local_step(): pl.pallas_call(functools.partial(exchange_kernel, n, rows, group), out_sh...]
where the time goes in v4:
time: 51.7 us; the launch traced here: 51.6 us
  Pallas kernels  50.9 us (98%)
  between operations  0.64 us (1%)
    pallas_call x1, Pallas kernels, local_step(): pl.pallas_call(functools.partial(exchange_kernel, n, rows, group), out_sh...  49.6 us
    pallas_call x1, Pallas kernels, local_step(): pl.pallas_call(functools.partial(store_kernel, parts), out_shape=(jax.Sha...  1.36 us

profile of v4, /device:TPU:1, one launch (start us, length us, event | category | flops | bytes accessed | tf_op | source)
XLA Modules:
  0.0 51.6 jit_solution(14276651766209103884)
XLA Ops:
  0.6 49.6 %exchange.1 = (f32[16,32768]{1,0:T(8,128)S(1)}, f32[16,128]{1,0:T(8,128)S(1)}) custom-call(bf16[2048,12288]{1,0:T(8,128)(2,1)} %hidden.1, bf16[12288,256]{1,0:T(8,128)(2,1)} %w.1, f32[16,128]{1,0:T(8,128)} %bitcast.3, s32[16,128]{1,0:T(8,128)} %bitcast.4), custom_call_target="tpu_custom_call" | custom-call | tf_op jit(solution)/shard_map/exchange/pallas_call | solution.py:258
  50.2 1.4 %store.1 = (f32[16,32768]{1,0:T(8,128)}, f32[16,128]{1,0:T(8,128)}) custom-call(f32[16,32768]{1,0:T(8,128)S(1)} %get-tuple-element.6.table, f32[16,128]{1,0:T(8,128)S(1)} %get-tuple-element.7.tgt), custom_call_target="tpu_custom_call" | custom-call | tf_op jit(solution)/shard_map/store/pallas_call | solution.py:295

commit v5 on v4

--- a/solution.py
+++ b/solution.py
@@ -9,8 +9,8 @@
 
 MESH = pl.DeviceIdType.MESH
 SLOTS = 3
-FINE = ((1, 4), (3, 6), (5, 2))
-COARSE = (0, 2, 4, 6)
+FINE = ((1, 6), (3, 2), (5, 4))
+COARSE = (6, 4, 2, 0)
 TAKE = 2
 PACE = (1, 1)
 
@@ -24,9 +24,8 @@
 
 
 def exact_dot(x, ones_mask):
-    hi, mid, lo = split3(x)
-    dot = functools.partial(jnp.dot, preferred_element_type=jnp.float32)
-    return dot(lo, ones_mask) + dot(mid, ones_mask) + dot(hi, ones_mask)
+    three = jnp.concatenate(split3(x)[::-1], axis=1)
+    return jnp.dot(three, jnp.concatenate([ones_mask] * 3, axis=0), preferred_element_type=jnp.float32)
 
 
 def partners(me, step, steps, sign=1):
@@ -73,6 +72,11 @@
                 h_sem.at[slot],
             ).start()
 
+    fetch(0)
+    part = w.shape[0] // 4
+    for i in range(4):
+        at = pl.ds(i * part, part)
+        pltpu.make_async_copy(w.at[at], w_buf.at[at], w_sem).start()
     barrier = pltpu.get_barrier_semaphore()
 
     def greet(step, carry):
@@ -88,11 +92,6 @@
         return carry
 
     lax.fori_loop(0, steps, greet, 0)
-    fetch(0)
-    part = w.shape[0] // 4
-    for i in range(4):
-        at = pl.ds(i * part, part)
-        pltpu.make_async_copy(w.at[at], w_buf.at[at], w_sem).start()
     for s in range(1, SLOTS - 1):
         fetch(s)
     pltpu.make_async_copy(temp_hbm, temp, small_sem).start()

time: 51.7 us -> 49.5 us (0.957)
  Pallas kernels: 50.9 us -> 48.7 us
    pallas_call x1, Pallas kernels: 49.6 us -> 47.4 us  [local_step(): pl.pallas_call(functools.partial(exchange_kernel, n, rows, group), out_sh...]
where the time goes in v5:
time: 49.5 us; the launch traced here: 49.4 us
  Pallas kernels  48.7 us (98%)
  between operations  0.64 us (1%)
    pallas_call x1, Pallas kernels, local_step(): pl.pallas_call(functools.partial(exchange_kernel, n, rows, group), out_sh...  47.4 us
    pallas_call x1, Pallas kernels, local_step(): pl.pallas_call(functools.partial(store_kernel, parts), out_shape=(jax.Sha...  1.36 us

profile of v5, /device:TPU:1, one launch (start us, length us, event | category | flops | bytes accessed | tf_op | source)
XLA Modules:
  0.0 49.4 jit_solution(12150302669394647463)
XLA Ops:
  0.6 47.4 %exchange.1 = (f32[16,32768]{1,0:T(8,128)S(1)}, f32[16,128]{1,0:T(8,128)S(1)}) custom-call(bf16[2048,12288]{1,0:T(8,128)(2,1)} %hidden.1, bf16[12288,256]{1,0:T(8,128)(2,1)} %w.1, f32[16,128]{1,0:T(8,128)} %bitcast.3, s32[16,128]{1,0:T(8,128)} %bitcast.4), custom_call_target="tpu_custom_call" | custom-call | tf_op jit(solution)/shard_map/exchange/pallas_call | solution.py:257
  48.0 1.4 %store.1 = (f32[16,32768]{1,0:T(8,128)}, f32[16,128]{1,0:T(8,128)}) custom-call(f32[16,32768]{1,0:T(8,128)S(1)} %get-tuple-element.6.table, f32[16,128]{1,0:T(8,128)S(1)} %get-tuple-element.7.tgt), custom_call_target="tpu_custom_call" | custom-call | tf_op jit(solution)/shard_map/store/pallas_call | solution.py:294

commit v6 on v5

--- a/solution.py
+++ b/solution.py
@@ -9,7 +9,7 @@
 
 MESH = pl.DeviceIdType.MESH
 SLOTS = 3
-FINE = ((1, 6), (3, 2), (5, 4))
+FINE = ((1, 2), (3, 4), (5, 6))
 COARSE = (6, 4, 2, 0)
 TAKE = 2
 PACE = (1, 1)

time: 49.5 us -> 49.4 us (level)
  no operation moved by 1% of the time
where the time goes in v6:
time: 49.4 us; the launch traced here: 49.3 us
  Pallas kernels  48.7 us (99%)
  between operations  0.64 us (1%)
    pallas_call x1, Pallas kernels, local_step(): pl.pallas_call(functools.partial(exchange_kernel, n, rows, group), out_sh...  47.3 us
    pallas_call x1, Pallas kernels, local_step(): pl.pallas_call(functools.partial(store_kernel, parts), out_shape=(jax.Sha...  1.36 us

profile of v6, /device:TPU:1, one launch (start us, length us, event | category | flops | bytes accessed | tf_op | source)
XLA Modules:
  0.0 49.3 jit_solution(4973706784111917715)
XLA Ops:
  0.6 47.3 %exchange.1 = (f32[16,32768]{1,0:T(8,128)S(1)}, f32[16,128]{1,0:T(8,128)S(1)}) custom-call(bf16[2048,12288]{1,0:T(8,128)(2,1)} %hidden.1, bf16[12288,256]{1,0:T(8,128)(2,1)} %w.1, f32[16,128]{1,0:T(8,128)} %bitcast.3, s32[16,128]{1,0:T(8,128)} %bitcast.4), custom_call_target="tpu_custom_call" | custom-call | tf_op jit(solution)/shard_map/exchange/pallas_call | solution.py:257
  48.0 1.4 %store.1 = (f32[16,32768]{1,0:T(8,128)}, f32[16,128]{1,0:T(8,128)}) custom-call(f32[16,32768]{1,0:T(8,128)S(1)} %get-tuple-element.6.table, f32[16,128]{1,0:T(8,128)S(1)} %get-tuple-element.7.tgt), custom_call_target="tpu_custom_call" | custom-call | tf_op jit(solution)/shard_map/store/pallas_call | solution.py:294
